TPU v7x, 256 devices: a whole 4x4x8 slice. The times are simulated.
256 devices in a mesh: row: 32 (over x, z_lo, core), col: 8 (over z_hi, y).
Axes of the slice: x: 4, y: 4, z: 8 (z_hi: 2, z_lo: 4; z = z_hi * 4 + z_lo), core: 2. Of those that a mesh axis runs over, the one named last changes fastest.
Arguments:
- embed_first: bfloat16 [1536, 16384], P('col', 'row'), may hold values from -6 to 6
- embed_second: bfloat16 [1536, 16384], P('row', 'col'), may hold values from -6 to 6
- corr_grad: float32 [16384, 16384], P('row', 'col'), may hold values from -0.046875 to 0.046875
Outputs:
- grad_first: bfloat16 [1536, 16384], P('col', 'row')
- grad_second: bfloat16 [1536, 16384], P('row', 'col')
All inputs are finite; a program needn't handle non-finite values.
Results may differ from a plain program's by a relative error of at most 0.0065.
Values may be sent and summed in bfloat16 or wider, within the bound.
A program may use at most 128 MiB of HBM per device.

v0:
```python
import jax
import jax.numpy as jnp
from jax import lax
from jax.sharding import PartitionSpec as P


def cut_along(x, dim, peers):
    lengths = x.shape
    parts = x.reshape(*lengths[:dim], peers, lengths[dim] // peers, *lengths[dim + 1 :])
    return jnp.moveaxis(parts, dim, 0)


def sent_and_summed(x, axis, dim):
    peers = lax.axis_size(axis)
    parts = lax.all_to_all(cut_along(x, dim, peers), axis, 0, 0, tiled=True)
    return jnp.sum(parts.astype(jnp.float32), axis=0)


def local(embed_first, embed_second, corr_grad):
    low_grad = corr_grad.astype(jnp.bfloat16)
    first_terms = lax.dot_general(
        lax.all_gather(embed_second, "row", axis=0, tiled=True),
        low_grad,
        (((1,), (1,)), ((), ())),
        preferred_element_type=jnp.float32,
    )
    grad_first = sent_and_summed(first_terms.astype(jnp.bfloat16), "col", 0).astype(jnp.bfloat16)
    whole_first = lax.all_gather(embed_first, "col", axis=0, tiled=True)
    grad_second = sent_and_summed(
        jnp.dot(whole_first, low_grad, preferred_element_type=jnp.float32).astype(jnp.bfloat16),
        "row",
        0,
    ).astype(jnp.bfloat16)
    return (grad_first, grad_second)


def solution(mesh):
    return jax.shard_map(
        local,
        mesh=mesh,
        in_specs=(P("col", "row"), P("row", "col"), P("row", "col")),
        out_specs=(P("col", "row"), P("row", "col")),
        check_vma=False,
    )
```

profile of v0, /device:TPU:2, one launch (start us, length us, event | category | flops | bytes accessed | tf_op | source)
XLA Modules:
  0.0 316.0 jit_solution(858558997219356227)
XLA Ops:
  7.2 0.0 all-gather.5.cloned.1.call-start
  7.2 0.7 all-gather.5.cloned.1.call-update
  7.9 0.0 all-gather.3.cloned.1.call-start
  7.9 0.7 all-gather.3.cloned.1.call-update
  8.6 73.9 %all-gather.5.cloned.1.call-done = bf16[1536,512]{1,0:T(8,128)(2,1)} async-done(((bf16[192,512]{1,0:T(8,128)(2,1)}), bf16[1536,512]{1,0:T(8,128)(2,1)}) %all-gather.5.cloned.1.call-update) | async-done | bytes 1572880 | tf_op jit(solution)/shard_map/all_gather | solution.py:28
  82.6 8.8 %convolution_convert_fusion = bf16[1536,2048]{1,0:T(8,128)(2,1)} fusion(bf16[1536,512]{1,0:T(8,128)(2,1)} %all-gather.5.cloned.1.call-done, f32[512,2048]{1,0:T(8,128)} %param.5), kind=kOutput, calls=%fused_computation | convolution fusion | flops 3225419776 | bytes 12058624 | tf_op jit(solution)/shard_map/dot_general | solution.py:30
  91.3 5.3 %all-to-all-start.1 = ((bf16[32,48,2048]{2,1,0:T(8,128)(2,1)}), bf16[32,48,2048]{2,1,0:T(8,128)(2,1)}, u32[]{:S(2)}, u32[]{:S(2)}) async-start(bf16[32,48,2048]{2,1,0:T(8,128)(2,1)} %bitcast.4), calls=%async_computation.1 | async-start | bytes 12582912 | tf_op jit(solution)/shard_map/all_to_all | solution.py:15
  96.6 133.8 %all-gather.3.cloned.1.call-done = bf16[1536,2048]{1,0:T(8,128)(2,1)} async-done(((bf16[48,2048]{1,0:T(8,128)(2,1)}), bf16[1536,2048]{1,0:T(8,128)(2,1)}) %all-gather.3.cloned.1.call-update) | async-done | bytes 6291472 | tf_op jit(solution)/shard_map/all_gather | solution.py:22
  230.4 8.6 %convolution_convert_fusion.1 = bf16[1536,512]{1,0:T(8,128)(2,1)} fusion(bf16[1536,2048]{1,0:T(8,128)(2,1)} %all-gather.3.cloned.1.call-done, f32[512,2048]{1,0:T(8,128)} %param.5), kind=kOutput, calls=%fused_computation.1 | convolution fusion | flops 3223060480 | bytes 12058624 | tf_op jit(solution)/shard_map/dot_general | solution.py:21
  239.0 32.0 %all-to-all-done.1 = bf16[32,48,2048]{2,1,0:T(8,128)(2,1)} async-done(((bf16[32,48,2048]{2,1,0:T(8,128)(2,1)}), bf16[32,48,2048]{2,1,0:T(8,128)(2,1)}, u32[]{:S(2)}, u32[]{:S(2)}) %all-to-all-start.1) | async-done | bytes 6291488 | tf_op jit(solution)/shard_map/all_to_all | solution.py:15
  271.0 7.1 %all-to-all-start = ((bf16[8,192,512]{2,1,0:T(8,128)(2,1)}), bf16[8,192,512]{2,1,0:T(8,128)(2,1)S(1)}, u32[]{:S(2)}, u32[]{:S(2)}) async-start(bf16[8,192,512]{2,1,0:T(8,128)(2,1)} %bitcast), calls=%async_computation | async-start | bytes 3145728 | tf_op jit(solution)/shard_map/all_to_all | solution.py:15
  278.0 4.9 %reduce_sum.25 = bf16[48,2048]{1,0:T(8,128)(2,1)} reduce(bf16[32,48,2048]{2,1,0:T(8,128)(2,1)} %all-to-all-done.1, bf16[]{:T(256)} %constant.3.clone.1), dimensions={0}, to_apply=%region_1.0 | reduce | flops 3047424 | bytes 6488066 | tf_op jit(solution)/shard_map/reduce_sum | solution.py:16
  282.9 25.3 %all-to-all-done = bf16[8,192,512]{2,1,0:T(8,128)(2,1)S(1)} async-done(((bf16[8,192,512]{2,1,0:T(8,128)(2,1)}), bf16[8,192,512]{2,1,0:T(8,128)(2,1)S(1)}, u32[]{:S(2)}, u32[]{:S(2)}) %all-to-all-start) | async-done | bytes 1572896 | tf_op jit(solution)/shard_map/all_to_all | solution.py:15
  308.3 0.9 reduce_sum.24
Async XLA Ops:
  7.2 75.4 %all-gather.5.cloned.1.call-start = ((), (), s32[]{:S(2)}) async-start(), calls=%async_computation.3 | async-start | bytes 1769472 | tf_op jit(solution)/shard_map/all_gather | solution.py:28
  7.9 222.5 %all-gather.3.cloned.1.call-start = ((), (), s32[]{:S(2)}) async-start(), calls=%async_computation.2 | async-start | bytes 6488064 | tf_op jit(solution)/shard_map/all_gather | solution.py:22
  91.3 179.6 %all-to-all-start.1 = ((bf16[32,48,2048]{2,1,0:T(8,128)(2,1)}), bf16[32,48,2048]{2,1,0:T(8,128)(2,1)}, u32[]{:S(2)}, u32[]{:S(2)}) async-start(bf16[32,48,2048]{2,1,0:T(8,128)(2,1)} %bitcast.4), calls=%async_computation.1 | async-start | bytes 12582912 | tf_op jit(solution)/shard_map/all_to_all | solution.py:15
  271.0 37.3 %all-to-all-start = ((bf16[8,192,512]{2,1,0:T(8,128)(2,1)}), bf16[8,192,512]{2,1,0:T(8,128)(2,1)S(1)}, u32[]{:S(2)}, u32[]{:S(2)}) async-start(bf16[8,192,512]{2,1,0:T(8,128)(2,1)} %bitcast), calls=%async_computation | async-start | bytes 3145728 | tf_op jit(solution)/shard_map/all_to_all | solution.py:15
Sparse Core Ops, SparseCore 0:
  10.6 71.9 all-gather.4
  84.4 145.9 all-gather.2
where the time goes:
time: 316 us
  waiting for transfers between devices  266 us (84%)
  matrix products  17.4 us (6%)
  between operations  14 us (4%)
  starting transfers between devices  12.4 us (4%)
  other arithmetic  5.84 us (2%)
    all_gather x1, waiting for transfers between devices, local(): lax.all_gather(embed_second, 'row', axis=0, tiled=True)  134 us
    all_gather x1, waiting for transfers between devices, local(): whole_first = lax.all_gather(embed_first, 'col', axis=0, tiled=True)  73.9 us
    all_to_all x2, waiting for transfers between devices, sent_and_summed(): parts = lax.all_to_all(cut_along(x, dim, peers), axis, 0, 0, tiled=True)  57.3 us
    all_to_all x2, starting transfers between devices, sent_and_summed(): parts = lax.all_to_all(cut_along(x, dim, peers), axis, 0, 0, tiled=True)  12.3 us
    dot_general x1, matrix products, local(): jnp.dot(whole_first, low_grad, preferred_element_type=jnp.float32)  8.75 us
    dot_general x1, matrix products, local(): lax.dot_general(lax.all_gather(embed_second, 'row', axis=0, tiled=True),...  8.64 us
  transfers between devices with their start and end apart: 4, of which 4 were waited for; matrix products, arithmetic and copies ran while one was open for 7% of the time, Pallas kernels for 0%

commit v1 on v0

--- a/solution.py
+++ b/solution.py
@@ -2,6 +2,13 @@
 import jax.numpy as jnp
 from jax import lax
 from jax.sharding import PartitionSpec as P
+
+
+def swapped_in(x, mesh_axis, d):
+    size = lax.axis_size(mesh_axis)
+    blocks = jnp.stack([x for _ in range(size)])
+    blocks = lax.all_to_all(blocks, mesh_axis, split_axis=0, concat_axis=0)
+    return jnp.concatenate(blocks, axis=d)
 
 
 def cut_along(x, dim, peers):
@@ -25,7 +32,7 @@
         preferred_element_type=jnp.float32,
     )
     grad_first = sent_and_summed(first_terms.astype(jnp.bfloat16), "col", 0).astype(jnp.bfloat16)
-    whole_first = lax.all_gather(embed_first, "col", axis=0, tiled=True)
+    whole_first = swapped_in(embed_first, "col", 0)
     grad_second = sent_and_summed(
         jnp.dot(whole_first, low_grad, preferred_element_type=jnp.float32).astype(jnp.bfloat16),
         "row",

time: 316 us -> 285 us (0.902)
  waiting for transfers between devices: 266 us -> 207 us
  starting transfers between devices: 12.4 us -> 37.4 us
    all_gather x1, waiting for transfers between devices: 134 us -> 51.7 us  [local(): lax.all_gather(embed_second, 'row', axis=0, tiled=True)]
    all_gather x1 -> x0, waiting for transfers between devices: 73.9 us -> none  [local(): whole_first = lax.all_gather(embed_first, 'col', axis=0, tiled=True)]
    all_to_all x2, waiting for transfers between devices: 57.3 us -> 116 us  [sent_and_summed(): parts = lax.all_to_all(cut_along(x, dim, peers), axis, 0, 0, tiled=True)]
    all_to_all x0 -> x1, waiting for transfers between devices: none -> 38.6 us  [swapped_in(): blocks = lax.all_to_all(blocks, mesh_axis, split_axis=0, concat_axis=0)]
    all_to_all x2, starting transfers between devices: 12.3 us -> 26.2 us  [sent_and_summed(): parts = lax.all_to_all(cut_along(x, dim, peers), axis, 0, 0, tiled=True)]
    all_to_all x0 -> x1, starting transfers between devices: none -> 11.1 us  [swapped_in(): blocks = lax.all_to_all(blocks, mesh_axis, split_axis=0, concat_axis=0)]
where the time goes in v1:
time: 285 us; the launch traced here: 282 us
  waiting for transfers between devices  207 us (73%)
  starting transfers between devices  37.4 us (13%)
  matrix products  16.1 us (6%)
  between operations  14 us (5%)
  other arithmetic  5.84 us (2%)
    all_to_all x2, waiting for transfers between devices, sent_and_summed(): parts = lax.all_to_all(cut_along(x, dim, peers), axis, 0, 0, tiled=True)  116 us
    all_gather x1, waiting for transfers between devices, local(): lax.all_gather(embed_second, 'row', axis=0, tiled=True)  51.7 us
    all_to_all x1, waiting for transfers between devices, swapped_in(): blocks = lax.all_to_all(blocks, mesh_axis, split_axis=0, concat_axis=0)  38.6 us
    all_to_all x2, starting transfers between devices, sent_and_summed(): parts = lax.all_to_all(cut_along(x, dim, peers), axis, 0, 0, tiled=True)  26.2 us
    all_to_all x1, starting transfers between devices, swapped_in(): blocks = lax.all_to_all(blocks, mesh_axis, split_axis=0, concat_axis=0)  11.1 us
    dot_general x1, matrix products, local(): lax.dot_general(lax.all_gather(embed_second, 'row', axis=0, tiled=True),...  8.64 us
    dot_general x1, matrix products, local(): jnp.dot(whole_first, low_grad, preferred_element_type=jnp.float32)  7.47 us
    reduce_sum x2, other arithmetic, sent_and_summed(): return jnp.sum(parts.astype(jnp.float32), axis=0)  5.84 us
  transfers between devices with their start and end apart: 4, of which 4 were waited for; matrix products, arithmetic and copies ran while one was open for 7% of the time, Pallas kernels for 0%

profile of v1, /device:TPU:2, one launch (start us, length us, event | category | flops | bytes accessed | tf_op | source)
XLA Modules:
  0.0 282.3 jit_solution(3234890773814586554)
XLA Ops:
  7.2 2.2 stack.2
  9.4 11.1 %all-to-all-start.1 = ((bf16[8,192,512]{2,1,0:T(8,128)(2,1)}), bf16[8,192,512]{2,1,0:T(8,128)(2,1)S(1)}, u32[]{:S(2)}, u32[]{:S(2)}) async-start(bf16[8,192,512]{2,1,0:T(8,128)(2,1)} %stack.2), calls=%async_computation.1 | async-start | bytes 3145728 | tf_op jit(solution)/shard_map/all_to_all | solution.py:10
  20.5 0.0 all-gather.2.cloned.1.call-start
  20.5 0.7 all-gather.2.cloned.1.call-update
  21.2 38.6 %all-to-all-done.1 = bf16[8,192,512]{2,1,0:T(8,128)(2,1)S(1)} async-done(((bf16[8,192,512]{2,1,0:T(8,128)(2,1)}), bf16[8,192,512]{2,1,0:T(8,128)(2,1)S(1)}, u32[]{:S(2)}, u32[]{:S(2)}) %all-to-all-start.1) | async-done | bytes 1572896 | tf_op jit(solution)/shard_map/all_to_all | solution.py:10
  59.8 7.5 %convolution_convert_fusion = bf16[1536,2048]{1,0:T(8,128)(2,1)} fusion(bf16[1536,512]{1,0:T(8,128)(2,1)S(1)} %bitcast.6, f32[512,2048]{1,0:T(8,128)} %param.5), kind=kOutput, calls=%fused_computation | convolution fusion | flops 3225419776 | bytes 12058624 | tf_op jit(solution)/shard_map/dot_general | solution.py:37
  67.2 19.0 %all-to-all-start.2 = ((bf16[32,48,2048]{2,1,0:T(8,128)(2,1)}), bf16[32,48,2048]{2,1,0:T(8,128)(2,1)}, u32[]{:S(2)}, u32[]{:S(2)}) async-start(bf16[32,48,2048]{2,1,0:T(8,128)(2,1)} %bitcast.5), calls=%async_computation.2 | async-start | bytes 12582912 | tf_op jit(solution)/shard_map/all_to_all | solution.py:22
  86.3 51.7 %all-gather.2.cloned.1.call-done = bf16[1536,2048]{1,0:T(8,128)(2,1)} async-done(((bf16[48,2048]{1,0:T(8,128)(2,1)}), bf16[1536,2048]{1,0:T(8,128)(2,1)}) %all-gather.2.cloned.1.call-update) | async-done | bytes 6291472 | tf_op jit(solution)/shard_map/all_gather | solution.py:29
  137.9 8.6 %convolution_convert_fusion.1 = bf16[1536,512]{1,0:T(8,128)(2,1)} fusion(bf16[1536,2048]{1,0:T(8,128)(2,1)} %all-gather.2.cloned.1.call-done, f32[512,2048]{1,0:T(8,128)} %param.5), kind=kOutput, calls=%fused_computation.1 | convolution fusion | flops 3223060480 | bytes 12058624 | tf_op jit(solution)/shard_map/dot_general | solution.py:28
  146.6 94.5 %all-to-all-done.2 = bf16[32,48,2048]{2,1,0:T(8,128)(2,1)} async-done(((bf16[32,48,2048]{2,1,0:T(8,128)(2,1)}), bf16[32,48,2048]{2,1,0:T(8,128)(2,1)}, u32[]{:S(2)}, u32[]{:S(2)}) %all-to-all-start.2) | async-done | bytes 6291488 | tf_op jit(solution)/shard_map/all_to_all | solution.py:22
  241.1 7.2 %all-to-all-start = ((bf16[8,192,512]{2,1,0:T(8,128)(2,1)}), bf16[8,192,512]{2,1,0:T(8,128)(2,1)S(1)}, u32[]{:S(2)}, u32[]{:S(2)}) async-start(bf16[8,192,512]{2,1,0:T(8,128)(2,1)} %bitcast), calls=%async_computation | async-start | bytes 3145728 | tf_op jit(solution)/shard_map/all_to_all | solution.py:22
  248.3 4.9 %reduce_sum.25 = bf16[48,2048]{1,0:T(8,128)(2,1)} reduce(bf16[32,48,2048]{2,1,0:T(8,128)(2,1)} %all-to-all-done.2, bf16[]{:T(256)} %constant.3.clone.1), dimensions={0}, to_apply=%region_1.0 | reduce | flops 3047424 | bytes 6488066 | tf_op jit(solution)/shard_map/reduce_sum | solution.py:23
  253.2 21.3 %all-to-all-done = bf16[8,192,512]{2,1,0:T(8,128)(2,1)S(1)} async-done(((bf16[8,192,512]{2,1,0:T(8,128)(2,1)}), bf16[8,192,512]{2,1,0:T(8,128)(2,1)S(1)}, u32[]{:S(2)}, u32[]{:S(2)}) %all-to-all-start) | async-done | bytes 1572896 | tf_op jit(solution)/shard_map/all_to_all | solution.py:22
  274.5 0.9 reduce_sum.24
Async XLA Ops:
  9.4 50.4 %all-to-all-start.1 = ((bf16[8,192,512]{2,1,0:T(8,128)(2,1)}), bf16[8,192,512]{2,1,0:T(8,128)(2,1)S(1)}, u32[]{:S(2)}, u32[]{:S(2)}) async-start(bf16[8,192,512]{2,1,0:T(8,128)(2,1)} %stack.2), calls=%async_computation.1 | async-start | bytes 3145728 | tf_op jit(solution)/shard_map/all_to_all | solution.py:10
  20.5 117.5 %all-gather.2.cloned.1.call-start = ((), (), s32[]{:S(2)}) async-start(), calls=%async_computation.3 | async-start | bytes 6488064 | tf_op jit(solution)/shard_map/all_gather | solution.py:29
  67.2 173.8 %all-to-all-start.2 = ((bf16[32,48,2048]{2,1,0:T(8,128)(2,1)}), bf16[32,48,2048]{2,1,0:T(8,128)(2,1)}, u32[]{:S(2)}, u32[]{:S(2)}) async-start(bf16[32,48,2048]{2,1,0:T(8,128)(2,1)} %bitcast.5), calls=%async_computation.2 | async-start | bytes 12582912 | tf_op jit(solution)/shard_map/all_to_all | solution.py:22
  241.1 33.5 %all-to-all-start = ((bf16[8,192,512]{2,1,0:T(8,128)(2,1)}), bf16[8,192,512]{2,1,0:T(8,128)(2,1)S(1)}, u32[]{:S(2)}, u32[]{:S(2)}) async-start(bf16[8,192,512]{2,1,0:T(8,128)(2,1)} %bitcast), calls=%async_computation | async-start | bytes 3145728 | tf_op jit(solution)/shard_map/all_to_all | solution.py:22
Sparse Core Ops, SparseCore 0:
  23.1 114.7 all-gather.1
